TPU v7x, 32 devices: a whole 2x2x4 slice. The times are simulated.
32 devices in a mesh: head: 4 (over x, core), outer: 2 (over y), inner: 4 (over z).
Axes of the slice: x: 2, y: 2, z: 4, core: 2. Of those that a mesh axis runs over, the one named last changes fastest.
Arguments:
- queries: bfloat16 [8, 256, 4096], P(('outer', 'inner'), 'head'), may hold values from -120 to 120
- keys: bfloat16 [8, 256, 1024], P(('outer', 'inner'), 'head'), may hold values from -6 to 6
- values: bfloat16 [8, 256, 1024], P(('outer', 'inner'), 'head'), may hold values from -6 to 6
- doc_lengths: int32 [4], replicated, may hold values from 1 to 1024, 2048 in all
Outputs:
- attended: bfloat16 [8, 256, 4096], P(('outer', 'inner'), 'head')
Inputs may be any that keep to these rules, and one draw needn't show every extreme that they name: `doc_lengths`: the documents of the packed sequence in order, summing to 2048.
All inputs are finite; a program needn't handle non-finite values.
Results may differ from a plain program's by a relative error of at most 0.0044.
Values may be sent and summed in bfloat16 or wider, within the bound.
A program may use at most 64 MiB of HBM per device.

v0:
```python
import math
import jax
import jax.numpy as jnp
from jax import lax
from jax.sharding import PartitionSpec as P

HD = 128
MAXDOC = 4096
NEG_FILL = -1e30


def passed_along(block, axis, distance):
    devices = range(lax.axis_size(axis))
    route = [(i - distance, i) for i in devices if i - distance in devices]
    return lax.ppermute(block, axis, route)


def doc_index(positions, doc_lengths):
    ends = jnp.cumsum(doc_lengths)
    return jnp.sum((positions[:, None] >= ends[None, :]).astype(jnp.int32), axis=1)


def fold_block(state, key_block, value_block, offset, context):
    q_heads, q_pos, q_doc, rank, doc_lengths = context
    rows = key_block.shape[0]
    heads = key_block.shape[1] // HD
    k_pos = (rank - offset) * rows + jnp.arange(rows, dtype=jnp.int32)
    k_doc = doc_index(k_pos, doc_lengths)
    visible = (
        (k_pos[None, :] >= 0)
        & (k_pos[None, :] <= q_pos[:, None])
        & (k_doc[None, :] == q_doc[:, None])
    )
    k_heads = key_block.reshape(rows, heads, HD)
    v_heads = value_block.reshape(rows, heads, HD)
    scores = jnp.einsum("qgeh,kgh->geqk", q_heads, k_heads, preferred_element_type=jnp.float32) * (
        1.0 / math.sqrt(HD)
    )
    running, total, summed = state
    masked = jnp.where(visible[None, None], scores, NEG_FILL)
    peak = jnp.maximum(running, jnp.max(masked, axis=-1))
    factor = jnp.exp(running - peak)
    weights = jnp.where(visible[None, None], jnp.exp(scores - peak[..., None]), 0.0)
    total = total * factor + jnp.sum(weights, axis=-1)
    rounded = weights.astype(jnp.bfloat16)
    added = jnp.einsum("geqk,kgh->qgeh", rounded, v_heads, preferred_element_type=jnp.float32)
    summed = summed * jnp.transpose(factor, (2, 0, 1))[..., None] + added
    return (peak, total, summed)


def body(queries, keys, values, doc_lengths):
    q_local, k_local, v_local = (
        lax.all_to_all(queries, "head", split_axis=2, concat_axis=1, tiled=True),
        lax.all_to_all(keys, "head", split_axis=2, concat_axis=1, tiled=True),
        lax.all_to_all(values, "head", split_axis=2, concat_axis=1, tiled=True),
    )
    rows = q_local.shape[1]
    kv_heads = k_local.shape[2] // HD
    group = q_local.shape[2] // k_local.shape[2]
    q_heads = q_local[0].reshape(rows, kv_heads, group, HD)
    rank = lax.axis_index(("outer", "inner"))
    reach = min(MAXDOC // rows, lax.axis_size(("outer", "inner")) // 2)
    q_pos = rank * rows + jnp.arange(rows, dtype=jnp.int32)
    q_doc = doc_index(q_pos, doc_lengths)
    context = (q_heads, q_pos, q_doc, rank, doc_lengths)
    state = (
        jnp.full((kv_heads, group, rows), NEG_FILL, jnp.float32),
        jnp.zeros((kv_heads, group, rows), jnp.float32),
        jnp.zeros((rows, kv_heads, group, HD), jnp.float32),
    )

    def attend(state, key_block, value_block, offset):
        return fold_block(state, key_block, value_block, offset, context)

    state = attend(state, k_local[0], v_local[0], 0)
    key_window = k_local
    value_window = v_local
    held = 1
    while held < reach + 1:
        extra = min(held, reach + 1 - held)
        sent_keys, sent_values = passed_along(
            (key_window[held - extra :], value_window[held - extra :]), ("outer", "inner"), held
        )
        key_window = jnp.concatenate([sent_keys, key_window], axis=0)
        value_window = jnp.concatenate([sent_values, value_window], axis=0)
        held = held + extra

    def sweep(offset, carried):
        index = reach - offset
        key_block = lax.dynamic_index_in_dim(key_window, index, 0, keepdims=False)
        value_block = lax.dynamic_index_in_dim(value_window, index, 0, keepdims=False)
        return attend(carried, key_block, value_block, offset)

    state = lax.fori_loop(1, reach + 1, sweep, state)
    running, total, summed = state
    result = summed / jnp.transpose(total, (2, 0, 1))[..., None]
    attended = result.astype(jnp.bfloat16).reshape(1, rows, kv_heads * group * HD)
    return lax.all_to_all(attended, "head", split_axis=1, concat_axis=2, tiled=True)


def solution(mesh):
    placed = (
        P(("outer", "inner"), "head", None),
        P(("outer", "inner"), "head", None),
        P(("outer", "inner"), "head", None),
        P(),
    )
    return jax.shard_map(
        body,
        mesh=mesh,
        in_specs=placed,
        out_specs=P(("outer", "inner"), "head", None),
        check_vma=False,
    )
```

profile of v0, /device:TPU:4, one launch (start us, length us, event | category | flops | bytes accessed | tf_op | source)
XLA Modules:
  0.0 129.2 jit_solution(5051317125559907742)
XLA Ops:
  0.0 1.3 copy.102
  1.3 0.5 broadcast.232
  1.8 2.2 %reduce.1 = bf16[1024,64]{1,0:T(8,128)(2,1)S(1)} reduce(bf16[1024,1,64]{2,1,0:T(2,128)(2,1)S(1)} %bitcast.132, bf16[]{:T(256)} %broadcast.232), dimensions={1}, to_apply=%bitcast.73.reduce_sub_computation | reduce | bytes 262146
  4.0 0.9 reshape.228
  4.9 3.3 %all-to-all-start = ((bf16[4,2,8192]{2,1,0:T(2,128)(2,1)}), bf16[4,2,8192]{2,1,0:T(2,128)(2,1)S(1)}, u32[]{:S(2)}, u32[]{:S(2)}) async-start(bf16[4,2,8192]{2,1,0:T(2,128)(2,1)} %reshape.228), calls=%async_computation | async-start | bytes 262144 | tf_op jit(solution)/shard_map/all_to_all | solution.py:54
  8.3 2.8 %copy.105 = bf16[1,64,4096]{1,0,2:T(2,128)(2,1)S(1)} copy(bf16[1,64,4096]{2,1,0:T(8,128)(2,1)S(1)} %copy-done) | data formatting | bytes 1048576 | tf_op args[0]
  11.1 22.4 %reduce = bf16[4096,64]{1,0:T(8,128)(2,1)S(1)} reduce(bf16[4096,1,64]{2,1,0:T(2,128)(2,1)S(1)} %bitcast.124, bf16[]{:T(256)} %broadcast.232), dimensions={1}, to_apply=%bitcast.75.reduce_sub_computation | reduce | bytes 1048578
  33.5 1.6 %reshape.230 = bf16[4,2,32768]{2,1,0:T(2,128)(2,1)} reshape(bf16[4096,64]{1,0:T(8,128)(2,1)S(1)} %reduce) | data formatting | bytes 1048576
  35.5 2.2 %reduce.2 = bf16[1024,64]{1,0:T(8,128)(2,1)S(1)} reduce(bf16[1024,1,64]{2,1,0:T(2,128)(2,1)S(1)} %bitcast.133, bf16[]{:T(256)} %broadcast.232), dimensions={1}, to_apply=%bitcast.77.reduce_sub_computation | reduce | bytes 262146
  37.7 0.9 reshape.232
  38.9 3.3 %all-to-all-start.2 = ((bf16[4,2,8192]{2,1,0:T(2,128)(2,1)}), bf16[4,2,8192]{2,1,0:T(2,128)(2,1)S(1)}, u32[]{:S(2)}, u32[]{:S(2)}) async-start(bf16[4,2,8192]{2,1,0:T(2,128)(2,1)} %reshape.232), calls=%async_computation.2 | async-start | bytes 262144 | tf_op jit(solution)/shard_map/all_to_all | solution.py:55
  43.0 3.8 %all-to-all-done.2 = bf16[4,2,8192]{2,1,0:T(2,128)(2,1)S(1)} async-done(((bf16[4,2,8192]{2,1,0:T(2,128)(2,1)}), bf16[4,2,8192]{2,1,0:T(2,128)(2,1)S(1)}, u32[]{:S(2)}, u32[]{:S(2)}) %all-to-all-start.2) | async-done | bytes 131104 | tf_op jit(solution)/shard_map/all_to_all | solution.py:55
  46.8 3.5 %all-to-all-start.1 = ((bf16[4,2,32768]{2,1,0:T(2,128)(2,1)}), bf16[4,2,32768]{2,1,0:T(2,128)(2,1)S(1)}, u32[]{:S(2)}, u32[]{:S(2)}) async-start(bf16[4,2,32768]{2,1,0:T(2,128)(2,1)} %reshape.230), calls=%async_computation.1 | async-start | bytes 1048576 | tf_op jit(solution)/shard_map/all_to_all | solution.py:53
  51.0 3.5 %collective-permute-start.1 = (bf16[1,256,256]{2,1,0:T(8,128)(2,1)S(1)}, bf16[1,256,256]{2,1,0:T(8,128)(2,1)S(1)}, u32[]{:S(2)}, u32[]{:S(2)}) collective-permute-start(bf16[1,256,256]{2,1,0:T(8,128)(2,1)S(1)} %bitcast.135), channel_id=1, source_target_pairs={{0,1},{1,2},{2,3},{3,4},{4,5},{5,6},{6,7},{8,9},{9,10},{10,11},{11... | collective-permute-start | bytes 393224 | tf_op jit(solution)/shard_map/ppermute | solution.py:15
  54.5 3.5 %collective-permute-start.4 = (bf16[1,256,256]{2,1,0:T(8,128)(2,1)S(1)}, bf16[1,256,256]{2,1,0:T(8,128)(2,1)S(1)}, u32[]{:S(2)}, u32[]{:S(2)}) collective-permute-start(bf16[1,256,256]{2,1,0:T(8,128)(2,1)S(1)} %bitcast.139), channel_id=1, source_target_pairs={{0,1},{1,2},{2,3},{3,4},{4,5},{5,6},{6,7},{8,9},{9,10},{10,11},{11... | collective-permute-start | bytes 393224 | tf_op jit(solution)/shard_map/ppermute | solution.py:15
  58.2 0.7 reshape_squeeze.11
  58.9 1.3 collective-permute-start
  60.2 1.3 %collective-permute-start.3 = (bf16[1,256,256]{2,1,0:T(8,128)(2,1)S(1)}, bf16[1,256,256]{2,1,0:T(8,128)(2,1)S(1)}, u32[]{:S(2)}, u32[]{:S(2)}) collective-permute-start(bf16[1,256,256]{2,1,0:T(8,128)(2,1)S(1)} %bitcast.140), channel_id=1, source_target_pairs={{0,4},{1,5},{2,6},{3,7},{8,12},{9,13},{10,14},{11,15},{16,20},{17,... | collective-permute-start | bytes 393224 | tf_op jit(solution)/shard_map/ppermute | solution.py:15
  61.5 0.7 pad_maximum_fusion.2
  62.2 3.1 %collective-permute-start.2 = (bf16[2,256,256]{2,1,0:T(8,128)(2,1)}, bf16[2,256,256]{2,1,0:T(8,128)(2,1)}, u32[]{:S(2)}, u32[]{:S(2)}) collective-permute-start(bf16[2,256,256]{2,1,0:T(8,128)(2,1)} %pad_maximum_fusion.2), channel_id=1, source_target_pairs={{0,2},{1,3},{2,4},{3,5},{4,6},{5,7},{8,10},{9,11},{10,12},{11,13},... | collective-permute-start | bytes 786440 | tf_op jit(solution)/shard_map/ppermute | solution.py:15
  65.4 0.7 pad_maximum_fusion.3
  66.1 1.9 %collective-permute-start.5 = (bf16[2,256,256]{2,1,0:T(8,128)(2,1)}, bf16[2,256,256]{2,1,0:T(8,128)(2,1)}, u32[]{:S(2)}, u32[]{:S(2)}) collective-permute-start(bf16[2,256,256]{2,1,0:T(8,128)(2,1)} %pad_maximum_fusion.3), channel_id=1, source_target_pairs={{0,2},{1,3},{2,4},{3,5},{4,6},{5,7},{8,10},{9,11},{10,12},{11,13},... | collective-permute-start | bytes 786440 | tf_op jit(solution)/shard_map/ppermute | solution.py:15
  68.0 0.9 reshape.231
  68.9 2.3 %copy.106 = bf16[1,64,4096]{2,1,0:T(8,128)(2,1)S(1)} copy(bf16[1,64,4096]{1,0,2:T(2,128)(2,1)S(1)} %bitcast.123) | data formatting | bytes 1048576 | tf_op jit(solution)/shard_map/all_to_all | solution.py:53
  73.1 0.8 fusion.21
  74.0 0.9 copy.109
  75.2 11.6 %collective-permute-done.2 = bf16[2,256,256]{2,1,0:T(8,128)(2,1)} collective-permute-done((bf16[2,256,256]{2,1,0:T(8,128)(2,1)}, bf16[2,256,256]{2,1,0:T(8,128)(2,1)}, u32[]{:S(2)}, u32[]{:S(2)}) %collective-permute-start.2) | collective-permute-done | bytes 262176 | tf_op jit(solution)/shard_map/ppermute | solution.py:15
  86.8 1.9 %pad_maximum_fusion = bf16[5,256,256]{2,1,0:T(8,128)(2,1)} fusion(bf16[1,256,256]{2,1,0:T(8,128)(2,1)S(1)} %bitcast.138, bf16[1,256,256]{2,1,0:T(8,128)(2,1)S(1)} %collective-permute-done.1, bf16[2,256,256]{2,1,0:T(8,128)(2,1)} %collective-permute-done.2, bf16[1,256,256]{2,1,0:T(8,128)(2,1)} %collective-permute-done), kind=kLoop, calls=%fused_computation.40 | loop fusion | flops 983040 | bytes 1310720 | tf_op jit(solution)/shard_map/concatenate | solution.py:84
  88.7 2.9 %collective-permute-done.5 = bf16[2,256,256]{2,1,0:T(8,128)(2,1)} collective-permute-done((bf16[2,256,256]{2,1,0:T(8,128)(2,1)}, bf16[2,256,256]{2,1,0:T(8,128)(2,1)}, u32[]{:S(2)}, u32[]{:S(2)}) %collective-permute-start.5) | collective-permute-done | bytes 262176 | tf_op jit(solution)/shard_map/ppermute | solution.py:15
  91.6 1.9 %pad_maximum_fusion.1 = bf16[5,256,256]{2,1,0:T(8,128)(2,1)} fusion(bf16[1,256,256]{2,1,0:T(8,128)(2,1)S(1)} %bitcast.142, bf16[1,256,256]{2,1,0:T(8,128)(2,1)S(1)} %collective-permute-done.4, bf16[2,256,256]{2,1,0:T(8,128)(2,1)} %collective-permute-done.5, bf16[1,256,256]{2,1,0:T(8,128)(2,1)S(1)} %collective-permute-done.3), kind=kLoop, calls=%fused_computation.41 | loop fusion | flops 983040 | bytes 1310720 | tf_op jit(solution)/shard_map/concatenate | solution.py:85
  93.5 17.5 %while.20 = (s32[]{:T(128)}, f32[2,4,256]{2,1,0:T(4,128)S(1)}, f32[2,4,256]{2,1,0:T(4,128)S(1)}, f32[256,2,4,128]{0,3,2,1:T(8,128)S(1)}, s32[]{:T(128)}, /*index...) while((s32[]{:T(128)}, f32[2,4,256]{2,1,0:T(4,128)S(1)}, ...), condition=%wide.region_8.9_spmd.clone, body=%wide.region_4.0_spmd.clone.sunk | while | flops 274999040 | bytes 10625787 | solution.py:94
  93.8 1.0 constant_dynamic-slice_fusion.3
  94.9 1.6 %fusion.50 = (f32[2,4,256]{2,1,0:T(4,128)S(1)}, f32[2,256,256,4]{2,1,3,0:T(8,128)S(1)}) fusion(pred[256,256]{0,1:T(8,128)(4,1)S(1)} %compare_and_fusion.3, bf16[256,2,128,1]{0,2,3,1:T(8,128)(2,1)S(1)} %bitcast.121, bf16[256,2,4,128]{3,0,2,1:T(8,128)(2,1)} %get-tuple-element.533), kind=kOutput, calls=%fused_computation.3.clone.1 | convolution fusion | flops 135788544 | bytes 2826240 | tf_op jit(solution)/shard_map/while/body/eval_jaxpr/qgeh,kgh->geqk/dot_general | solution.py:36
  96.6 0.8 fusion.53
  98.1 1.0 constant_dynamic-slice_fusion.3
  99.2 1.6 %fusion.50 = (f32[2,4,256]{2,1,0:T(4,128)S(1)}, f32[2,256,256,4]{2,1,3,0:T(8,128)S(1)}) fusion(pred[256,256]{0,1:T(8,128)(4,1)S(1)} %compare_and_fusion.3, bf16[256,2,128,1]{0,2,3,1:T(8,128)(2,1)S(1)} %bitcast.121, bf16[256,2,4,128]{3,0,2,1:T(8,128)(2,1)} %get-tuple-element.533), kind=kOutput, calls=%fused_computation.3.clone.1 | convolution fusion | flops 135788544 | bytes 2826240 | tf_op jit(solution)/shard_map/while/body/eval_jaxpr/qgeh,kgh->geqk/dot_general | solution.py:36
  101.0 0.8 fusion.53
  102.5 1.0 constant_dynamic-slice_fusion.3
  103.6 1.6 %fusion.50 = (f32[2,4,256]{2,1,0:T(4,128)S(1)}, f32[2,256,256,4]{2,1,3,0:T(8,128)S(1)}) fusion(pred[256,256]{0,1:T(8,128)(4,1)S(1)} %compare_and_fusion.3, bf16[256,2,128,1]{0,2,3,1:T(8,128)(2,1)S(1)} %bitcast.121, bf16[256,2,4,128]{3,0,2,1:T(8,128)(2,1)} %get-tuple-element.533), kind=kOutput, calls=%fused_computation.3.clone.1 | convolution fusion | flops 135788544 | bytes 2826240 | tf_op jit(solution)/shard_map/while/body/eval_jaxpr/qgeh,kgh->geqk/dot_general | solution.py:36
  105.3 0.8 fusion.53
  106.9 1.0 constant_dynamic-slice_fusion.3
  108.0 1.6 %fusion.50 = (f32[2,4,256]{2,1,0:T(4,128)S(1)}, f32[2,256,256,4]{2,1,3,0:T(8,128)S(1)}) fusion(pred[256,256]{0,1:T(8,128)(4,1)S(1)} %compare_and_fusion.3, bf16[256,2,128,1]{0,2,3,1:T(8,128)(2,1)S(1)} %bitcast.121, bf16[256,2,4,128]{3,0,2,1:T(8,128)(2,1)} %get-tuple-element.533), kind=kOutput, calls=%fused_computation.3.clone.1 | convolution fusion | flops 135788544 | bytes 2826240 | tf_op jit(solution)/shard_map/while/body/eval_jaxpr/qgeh,kgh->geqk/dot_general | solution.py:36
  109.7 0.8 fusion.53
  111.1 1.0 copy.121
  112.1 3.7 %reduce.3 = bf16[256,1024]{1,0:T(8,128)(2,1)S(1)} reduce(bf16[256,1,1024]{2,1,0:T(2,128)(2,1)S(1)} %bitcast.127, bf16[]{:T(256)} %broadcast.232), dimensions={1}, to_apply=%bitcast.79.reduce_sub_computation | reduce | bytes 1048578
  116.1 11.5 %all_to_all.69 = bf16[4,2,32768]{2,1,0:T(2,128)(2,1)S(1)} all-to-all(bf16[4,2,32768]{2,1,0:T(2,128)(2,1)S(1)} %reshape.234), channel_id=1, replica_groups=mesh['head'=4,'outer'=2,'inner'=4] {'head'}, dimensions={0} | all-to-all | bytes 1048576 | tf_op jit(solution)/shard_map/all_to_all | solution.py:98
  127.6 0.5 reshape.235
  128.3 0.8 copy.138
  (80 shorter events, 9.0 us)
Async XLA Ops:
  0.0 8.3 %copy-start = (bf16[1,64,4096]{2,1,0:T(8,128)(2,1)S(1)}, bf16[1,64,4096]{2,1,0:T(8,128)(2,1)}, u32[]{:S(2)}) copy-start(bf16[1,64,4096]{2,1,0:T(8,128)(2,1)} %param.6) | copy-start | bytes 1572868
  4.9 33.9 %all-to-all-start = ((bf16[4,2,8192]{2,1,0:T(2,128)(2,1)}), bf16[4,2,8192]{2,1,0:T(2,128)(2,1)S(1)}, u32[]{:S(2)}, u32[]{:S(2)}) async-start(bf16[4,2,8192]{2,1,0:T(2,128)(2,1)} %reshape.228), calls=%async_computation | async-start | bytes 262144 | tf_op jit(solution)/shard_map/all_to_all | solution.py:54
  11.1 24.0 %copy-start.1 = (bf16[1,64,1024]{2,1,0:T(8,128)(2,1)S(1)}, bf16[1,64,1024]{2,1,0:T(8,128)(2,1)}, u32[]{:S(2)}) copy-start(bf16[1,64,1024]{2,1,0:T(8,128)(2,1)} %param.8) | copy-start | bytes 393220
  33.5 5.1 %copy-start.3 = (s32[4]{0:T(128)S(1)}, s32[4]{0:T(128)}, u32[]{:S(2)}) copy-start(s32[4]{0:T(128)} %param.9) | copy-start | bytes 52
  38.9 7.9 %all-to-all-start.2 = ((bf16[4,2,8192]{2,1,0:T(2,128)(2,1)}), bf16[4,2,8192]{2,1,0:T(2,128)(2,1)S(1)}, u32[]{:S(2)}, u32[]{:S(2)}) async-start(bf16[4,2,8192]{2,1,0:T(2,128)(2,1)} %reshape.232), calls=%async_computation.2 | async-start | bytes 262144 | tf_op jit(solution)/shard_map/all_to_all | solution.py:55
  46.8 21.2 %all-to-all-start.1 = ((bf16[4,2,32768]{2,1,0:T(2,128)(2,1)}), bf16[4,2,32768]{2,1,0:T(2,128)(2,1)S(1)}, u32[]{:S(2)}, u32[]{:S(2)}) async-start(bf16[4,2,32768]{2,1,0:T(2,128)(2,1)} %reshape.230), calls=%async_computation.1 | async-start | bytes 1048576 | tf_op jit(solution)/shard_map/all_to_all | solution.py:53
  51.0 10.5 %collective-permute-start.1 = (bf16[1,256,256]{2,1,0:T(8,128)(2,1)S(1)}, bf16[1,256,256]{2,1,0:T(8,128)(2,1)S(1)}, u32[]{:S(2)}, u32[]{:S(2)}) collective-permute-start(bf16[1,256,256]{2,1,0:T(8,128)(2,1)S(1)} %bitcast.135), channel_id=1, source_target_pairs={{0,1},{1,2},{2,3},{3,4},{4,5},{5,6},{6,7},{8,9},{9,10},{10,11},{11... | collective-permute-start | bytes 393224 | tf_op jit(solution)/shard_map/ppermute | solution.py:15
  54.5 10.8 %collective-permute-start.4 = (bf16[1,256,256]{2,1,0:T(8,128)(2,1)S(1)}, bf16[1,256,256]{2,1,0:T(8,128)(2,1)S(1)}, u32[]{:S(2)}, u32[]{:S(2)}) collective-permute-start(bf16[1,256,256]{2,1,0:T(8,128)(2,1)S(1)} %bitcast.139), channel_id=1, source_target_pairs={{0,1},{1,2},{2,3},{3,4},{4,5},{5,6},{6,7},{8,9},{9,10},{10,11},{11... | collective-permute-start | bytes 393224 | tf_op jit(solution)/shard_map/ppermute | solution.py:15
  58.9 16.3 %collective-permute-start = (bf16[1,256,256]{2,1,0:T(8,128)(2,1)S(1)}, bf16[1,256,256]{2,1,0:T(8,128)(2,1)}, u32[]{:S(2)}, u32[]{:S(2)}) collective-permute-start(bf16[1,256,256]{2,1,0:T(8,128)(2,1)S(1)} %bitcast.136), channel_id=1, source_target_pairs={{0,4},{1,5},{2,6},{3,7},{8,12},{9,13},{10,14},{11,15},{16,20},{17,... | collective-permute-start | bytes 393224 | tf_op jit(solution)/shard_map/ppermute | solution.py:15
  60.2 28.5 %collective-permute-start.3 = (bf16[1,256,256]{2,1,0:T(8,128)(2,1)S(1)}, bf16[1,256,256]{2,1,0:T(8,128)(2,1)S(1)}, u32[]{:S(2)}, u32[]{:S(2)}) collective-permute-start(bf16[1,256,256]{2,1,0:T(8,128)(2,1)S(1)} %bitcast.140), channel_id=1, source_target_pairs={{0,4},{1,5},{2,6},{3,7},{8,12},{9,13},{10,14},{11,15},{16,20},{17,... | collective-permute-start | bytes 393224 | tf_op jit(solution)/shard_map/ppermute | solution.py:15
  62.2 24.6 %collective-permute-start.2 = (bf16[2,256,256]{2,1,0:T(8,128)(2,1)}, bf16[2,256,256]{2,1,0:T(8,128)(2,1)}, u32[]{:S(2)}, u32[]{:S(2)}) collective-permute-start(bf16[2,256,256]{2,1,0:T(8,128)(2,1)} %pad_maximum_fusion.2), channel_id=1, source_target_pairs={{0,2},{1,3},{2,4},{3,5},{4,6},{5,7},{8,10},{9,11},{10,12},{11,13},... | collective-permute-start | bytes 786440 | tf_op jit(solution)/shard_map/ppermute | solution.py:15
  66.1 25.5 %collective-permute-start.5 = (bf16[2,256,256]{2,1,0:T(8,128)(2,1)}, bf16[2,256,256]{2,1,0:T(8,128)(2,1)}, u32[]{:S(2)}, u32[]{:S(2)}) collective-permute-start(bf16[2,256,256]{2,1,0:T(8,128)(2,1)} %pad_maximum_fusion.3), channel_id=1, source_target_pairs={{0,2},{1,3},{2,4},{3,5},{4,6},{5,7},{8,10},{9,11},{10,12},{11,13},... | collective-permute-start | bytes 786440 | tf_op jit(solution)/shard_map/ppermute | solution.py:15
  72.1 1.0 copy-start.2
where the time goes:
time: 130 us; the launch traced here: 129 us
  other arithmetic  39.8 us (31%)
  starting transfers between devices  24.7 us (19%)
  local copies, waits for them, and re-layouts  23.5 us (18%)
  waiting for transfers between devices  18.3 us (14%)
  blocking collectives  11.5 us (9%)
  matrix products  10.7 us (8%)
    unnamed x4, other arithmetic  30.5 us
    ppermute x6, starting transfers between devices, passed_along(): return lax.ppermute(block, axis, route)  14.6 us
    ppermute x6, waiting for transfers between devices, passed_along(): return lax.ppermute(block, axis, route)  14.5 us
    all_to_all x1, blocking collectives, body(): lax.all_to_all(attended, 'head', split_axis=1, concat_axis=2, tiled=True)  11.5 us
    unnamed x22, local copies, waits for them, and re-layouts  11.3 us
    dot_general x5, matrix products, fold_block(): jnp.einsum('qgeh,kgh->geqk', q_heads, k_heads, preferred_element_type=jnp...  6.84 us
    dynamic_slice x8, local copies, waits for them, and re-layouts, sweep(): lax.dynamic_index_in_dim(value_window, index, 0, keepdims=False)  4.36 us
    dot_general x5, matrix products, fold_block(): jnp.einsum('geqk,kgh->qgeh', rounded, v_heads, preferred_element_type=jnp...  3.91 us
  transfers between devices with their start and end apart: 9, of which 3 were waited for; matrix products, arithmetic and copies ran while one was open for 33% of the time, Pallas kernels for 0%

commit v1 on v0

--- a/solution.py
+++ b/solution.py
@@ -95,7 +95,10 @@
     running, total, summed = state
     result = summed / jnp.transpose(total, (2, 0, 1))[..., None]
     attended = result.astype(jnp.bfloat16).reshape(1, rows, kv_heads * group * HD)
-    return lax.all_to_all(attended, "head", split_axis=1, concat_axis=2, tiled=True)
+    return jnp.concatenate(
+        lax.all_to_all(jnp.stack(jnp.split(attended, lax.axis_size("head"), axis=1)), "head", 0, 0),
+        axis=2,
+    )
 
 
 def solution(mesh):

time: 130 us -> 125 us (0.962)
  other arithmetic: 39.8 us -> 36 us
  local copies, waits for them, and re-layouts: 23.5 us -> 22.1 us
    unnamed x4 -> x3, other arithmetic: 30.5 us -> 26.7 us
    unnamed x22 -> x23, local copies, waits for them, and re-layouts: 11.3 us -> 10.7 us
  transfers between devices with their start and end apart: 9 -> 9, of which waited for: 3 -> 3; matrix products, arithmetic and copies ran while one was open for 33% -> 34% of each run, Pallas kernels for 0% -> 0%
where the time goes in v1:
time: 125 us; the launch traced here: 124 us
  other arithmetic  36 us (29%)
  starting transfers between devices  24.7 us (20%)
  local copies, waits for them, and re-layouts  22.1 us (18%)
  waiting for transfers between devices  18.3 us (15%)
  blocking collectives  11.5 us (9%)
  matrix products  10.7 us (9%)
    unnamed x3, other arithmetic  26.7 us
    ppermute x6, starting transfers between devices, passed_along(): return lax.ppermute(block, axis, route)  14.6 us
    ppermute x6, waiting for transfers between devices, passed_along(): return lax.ppermute(block, axis, route)  14.5 us
    all_to_all x1, blocking collectives, body(): lax.all_to_all(jnp.stack(jnp.split(attended, lax.axis_size('head'), axis=...  11.5 us
    unnamed x23, local copies, waits for them, and re-layouts  10.7 us
    dot_general x5, matrix products, fold_block(): jnp.einsum('qgeh,kgh->geqk', q_heads, k_heads, preferred_element_type=jnp...  6.83 us
    dynamic_slice x8, local copies, waits for them, and re-layouts, sweep(): lax.dynamic_index_in_dim(value_window, index, 0, keepdims=False)  4.36 us
    dot_general x5, matrix products, fold_block(): jnp.einsum('geqk,kgh->qgeh', rounded, v_heads, preferred_element_type=jnp...  3.91 us
  transfers between devices with their start and end apart: 9, of which 3 were waited for; matrix products, arithmetic and copies ran while one was open for 34% of the time, Pallas kernels for 0%

profile of v1, /device:TPU:4, one launch (start us, length us, event | category | flops | bytes accessed | tf_op | source)
XLA Modules:
  0.0 124.1 jit_solution(10724036115716719562)
XLA Ops:
  0.0 1.3 %copy.106 = bf16[1,64,1024]{1,0,2:T(2,128)(2,1)S(1)} copy(bf16[1,64,1024]{2,1,0:T(8,128)(2,1)} %param.7) | data formatting | bytes 262144 | tf_op args[1]
  1.3 0.5 broadcast.232
  1.8 2.2 %reduce.1 = bf16[1024,64]{1,0:T(8,128)(2,1)S(1)} reduce(bf16[1024,1,64]{2,1,0:T(2,128)(2,1)S(1)} %bitcast.129, bf16[]{:T(256)} %broadcast.232), dimensions={1}, to_apply=%bitcast.75.reduce_sub_computation | reduce | bytes 262146
  4.0 0.9 reshape.236
  4.8 3.3 %all-to-all-start = ((bf16[4,2,8192]{2,1,0:T(2,128)(2,1)}), bf16[4,2,8192]{2,1,0:T(2,128)(2,1)S(1)}, u32[]{:S(2)}, u32[]{:S(2)}) async-start(bf16[4,2,8192]{2,1,0:T(2,128)(2,1)} %reshape.236), calls=%async_computation | async-start | bytes 262144 | tf_op jit(solution)/shard_map/all_to_all | solution.py:54
  8.2 2.8 %copy.109 = bf16[1,64,4096]{1,0,2:T(2,128)(2,1)S(1)} copy(bf16[1,64,4096]{2,1,0:T(8,128)(2,1)S(1)} %copy-done) | data formatting | bytes 1048576 | tf_op args[0]
  11.0 22.4 %reduce = bf16[4096,64]{1,0:T(8,128)(2,1)S(1)} reduce(bf16[4096,1,64]{2,1,0:T(2,128)(2,1)S(1)} %bitcast.124, bf16[]{:T(256)} %broadcast.232), dimensions={1}, to_apply=%bitcast.77.reduce_sub_computation | reduce | bytes 1048578
  33.4 1.6 %reshape.238 = bf16[4,2,32768]{2,1,0:T(2,128)(2,1)} reshape(bf16[4096,64]{1,0:T(8,128)(2,1)S(1)} %reduce) | data formatting | bytes 1048576
  35.3 2.2 %reduce.2 = bf16[1024,64]{1,0:T(8,128)(2,1)S(1)} reduce(bf16[1024,1,64]{2,1,0:T(2,128)(2,1)S(1)} %bitcast.130, bf16[]{:T(256)} %broadcast.232), dimensions={1}, to_apply=%bitcast.79.reduce_sub_computation | reduce | bytes 262146
  37.5 0.9 reshape.240
  38.7 3.3 %all-to-all-start.2 = ((bf16[4,2,8192]{2,1,0:T(2,128)(2,1)}), bf16[4,2,8192]{2,1,0:T(2,128)(2,1)S(1)}, u32[]{:S(2)}, u32[]{:S(2)}) async-start(bf16[4,2,8192]{2,1,0:T(2,128)(2,1)} %reshape.240), calls=%async_computation.2 | async-start | bytes 262144 | tf_op jit(solution)/shard_map/all_to_all | solution.py:55
  42.8 3.8 %all-to-all-done.2 = bf16[4,2,8192]{2,1,0:T(2,128)(2,1)S(1)} async-done(((bf16[4,2,8192]{2,1,0:T(2,128)(2,1)}), bf16[4,2,8192]{2,1,0:T(2,128)(2,1)S(1)}, u32[]{:S(2)}, u32[]{:S(2)}) %all-to-all-start.2) | async-done | bytes 131104 | tf_op jit(solution)/shard_map/all_to_all | solution.py:55
  46.6 3.5 %all-to-all-start.1 = ((bf16[4,2,32768]{2,1,0:T(2,128)(2,1)}), bf16[4,2,32768]{2,1,0:T(2,128)(2,1)S(1)}, u32[]{:S(2)}, u32[]{:S(2)}) async-start(bf16[4,2,32768]{2,1,0:T(2,128)(2,1)} %reshape.238), calls=%async_computation.1 | async-start | bytes 1048576 | tf_op jit(solution)/shard_map/all_to_all | solution.py:53
  50.8 3.5 %collective-permute-start.1 = (bf16[1,256,256]{2,1,0:T(8,128)(2,1)S(1)}, bf16[1,256,256]{2,1,0:T(8,128)(2,1)S(1)}, u32[]{:S(2)}, u32[]{:S(2)}) collective-permute-start(bf16[1,256,256]{2,1,0:T(8,128)(2,1)S(1)} %bitcast.133), channel_id=1, source_target_pairs={{0,1},{1,2},{2,3},{3,4},{4,5},{5,6},{6,7},{8,9},{9,10},{10,11},{11... | collective-permute-start | bytes 393224 | tf_op jit(solution)/shard_map/ppermute | solution.py:15
  54.3 3.5 %collective-permute-start.4 = (bf16[1,256,256]{2,1,0:T(8,128)(2,1)S(1)}, bf16[1,256,256]{2,1,0:T(8,128)(2,1)S(1)}, u32[]{:S(2)}, u32[]{:S(2)}) collective-permute-start(bf16[1,256,256]{2,1,0:T(8,128)(2,1)S(1)} %bitcast.137), channel_id=1, source_target_pairs={{0,1},{1,2},{2,3},{3,4},{4,5},{5,6},{6,7},{8,9},{9,10},{10,11},{11... | collective-permute-start | bytes 393224 | tf_op jit(solution)/shard_map/ppermute | solution.py:15
  58.0 0.7 reshape_squeeze.11
  58.7 1.3 %collective-permute-start = (bf16[1,256,256]{2,1,0:T(8,128)(2,1)S(1)}, bf16[1,256,256]{2,1,0:T(8,128)(2,1)}, u32[]{:S(2)}, u32[]{:S(2)}) collective-permute-start(bf16[1,256,256]{2,1,0:T(8,128)(2,1)S(1)} %bitcast.134), channel_id=1, source_target_pairs={{0,4},{1,5},{2,6},{3,7},{8,12},{9,13},{10,14},{11,15},{16,20},{17,... | collective-permute-start | bytes 393224 | tf_op jit(solution)/shard_map/ppermute | solution.py:15
  60.0 1.3 %collective-permute-start.3 = (bf16[1,256,256]{2,1,0:T(8,128)(2,1)S(1)}, bf16[1,256,256]{2,1,0:T(8,128)(2,1)S(1)}, u32[]{:S(2)}, u32[]{:S(2)}) collective-permute-start(bf16[1,256,256]{2,1,0:T(8,128)(2,1)S(1)} %bitcast.138), channel_id=1, source_target_pairs={{0,4},{1,5},{2,6},{3,7},{8,12},{9,13},{10,14},{11,15},{16,20},{17,... | collective-permute-start | bytes 393224 | tf_op jit(solution)/shard_map/ppermute | solution.py:15
  61.3 0.7 pad_maximum_fusion.3
  62.1 3.1 %collective-permute-start.2 = (bf16[2,256,256]{2,1,0:T(8,128)(2,1)}, bf16[2,256,256]{2,1,0:T(8,128)(2,1)}, u32[]{:S(2)}, u32[]{:S(2)}) collective-permute-start(bf16[2,256,256]{2,1,0:T(8,128)(2,1)} %pad_maximum_fusion.3), channel_id=1, source_target_pairs={{0,2},{1,3},{2,4},{3,5},{4,6},{5,7},{8,10},{9,11},{10,12},{11,13},... | collective-permute-start | bytes 786440 | tf_op jit(solution)/shard_map/ppermute | solution.py:15
  65.2 0.7 pad_maximum_fusion.4
  65.9 1.9 %collective-permute-start.5 = (bf16[2,256,256]{2,1,0:T(8,128)(2,1)}, bf16[2,256,256]{2,1,0:T(8,128)(2,1)}, u32[]{:S(2)}, u32[]{:S(2)}) collective-permute-start(bf16[2,256,256]{2,1,0:T(8,128)(2,1)} %pad_maximum_fusion.4), channel_id=1, source_target_pairs={{0,2},{1,3},{2,4},{3,5},{4,6},{5,7},{8,10},{9,11},{10,12},{11,13},... | collective-permute-start | bytes 786440 | tf_op jit(solution)/shard_map/ppermute | solution.py:15
  67.8 0.9 reshape.239
  68.7 2.3 %copy.110 = bf16[1,64,4096]{2,1,0:T(8,128)(2,1)S(1)} copy(bf16[1,64,4096]{1,0,2:T(2,128)(2,1)S(1)} %bitcast.123) | data formatting | bytes 1048576 | tf_op jit(solution)/shard_map/all_to_all | solution.py:53
  71.9 0.5 fusion.16
  72.5 0.5 fusion.20
  73.0 0.8 fusion.21
  73.8 0.9 copy.113
  75.0 11.6 %collective-permute-done.2 = bf16[2,256,256]{2,1,0:T(8,128)(2,1)} collective-permute-done((bf16[2,256,256]{2,1,0:T(8,128)(2,1)}, bf16[2,256,256]{2,1,0:T(8,128)(2,1)}, u32[]{:S(2)}, u32[]{:S(2)}) %collective-permute-start.2) | collective-permute-done | bytes 262176 | tf_op jit(solution)/shard_map/ppermute | solution.py:15
  86.6 1.9 %pad_maximum_fusion = bf16[5,256,256]{2,1,0:T(8,128)(2,1)} fusion(bf16[1,256,256]{2,1,0:T(8,128)(2,1)S(1)} %bitcast.136, bf16[1,256,256]{2,1,0:T(8,128)(2,1)S(1)} %collective-permute-done.1, bf16[2,256,256]{2,1,0:T(8,128)(2,1)} %collective-permute-done.2, bf16[1,256,256]{2,1,0:T(8,128)(2,1)} %collective-permute-done), kind=kLoop, calls=%fused_computation.40 | loop fusion | flops 983040 | bytes 1310720 | tf_op jit(solution)/shard_map/concatenate | solution.py:84
  88.5 2.9 %collective-permute-done.5 = bf16[2,256,256]{2,1,0:T(8,128)(2,1)} collective-permute-done((bf16[2,256,256]{2,1,0:T(8,128)(2,1)}, bf16[2,256,256]{2,1,0:T(8,128)(2,1)}, u32[]{:S(2)}, u32[]{:S(2)}) %collective-permute-start.5) | collective-permute-done | bytes 262176 | tf_op jit(solution)/shard_map/ppermute | solution.py:15
  91.4 1.9 %pad_maximum_fusion.1 = bf16[5,256,256]{2,1,0:T(8,128)(2,1)} fusion(bf16[1,256,256]{2,1,0:T(8,128)(2,1)S(1)} %bitcast.140, bf16[1,256,256]{2,1,0:T(8,128)(2,1)S(1)} %collective-permute-done.4, bf16[2,256,256]{2,1,0:T(8,128)(2,1)} %collective-permute-done.5, bf16[1,256,256]{2,1,0:T(8,128)(2,1)S(1)} %collective-permute-done.3), kind=kLoop, calls=%fused_computation.41 | loop fusion | flops 983040 | bytes 1310720 | tf_op jit(solution)/shard_map/concatenate | solution.py:85
  93.3 17.5 %while.20 = (s32[]{:T(128)}, f32[2,4,256]{2,1,0:T(4,128)S(1)}, f32[2,4,256]{2,1,0:T(4,128)S(1)}, f32[256,2,4,128]{0,3,2,1:T(8,128)S(1)}, s32[]{:T(128)}, /*index...) while((s32[]{:T(128)}, f32[2,4,256]{2,1,0:T(4,128)S(1)}, ...), condition=%wide.region_8.9_spmd.clone, body=%wide.region_4.0_spmd.clone.sunk | while | flops 274999040 | bytes 10625787 | solution.py:94
  93.6 1.0 constant_dynamic-slice_fusion.3
  94.7 1.6 %fusion.51 = (f32[2,4,256]{2,1,0:T(4,128)S(1)}, f32[2,256,256,4]{2,1,3,0:T(8,128)S(1)}) fusion(pred[256,256]{0,1:T(8,128)(4,1)S(1)} %compare_and_fusion.3, bf16[256,2,128,1]{0,2,3,1:T(8,128)(2,1)S(1)} %bitcast.121, bf16[256,2,4,128]{3,0,2,1:T(8,128)(2,1)} %get-tuple-element.537), kind=kOutput, calls=%fused_computation.3.clone.1 | convolution fusion | flops 135788544 | bytes 2826240 | tf_op jit(solution)/shard_map/while/body/eval_jaxpr/qgeh,kgh->geqk/dot_general | solution.py:36
  96.4 0.8 fusion.54
  98.0 1.0 constant_dynamic-slice_fusion.3
  99.1 1.6 %fusion.51 = (f32[2,4,256]{2,1,0:T(4,128)S(1)}, f32[2,256,256,4]{2,1,3,0:T(8,128)S(1)}) fusion(pred[256,256]{0,1:T(8,128)(4,1)S(1)} %compare_and_fusion.3, bf16[256,2,128,1]{0,2,3,1:T(8,128)(2,1)S(1)} %bitcast.121, bf16[256,2,4,128]{3,0,2,1:T(8,128)(2,1)} %get-tuple-element.537), kind=kOutput, calls=%fused_computation.3.clone.1 | convolution fusion | flops 135788544 | bytes 2826240 | tf_op jit(solution)/shard_map/while/body/eval_jaxpr/qgeh,kgh->geqk/dot_general | solution.py:36
  100.8 0.8 fusion.54
  102.3 1.0 constant_dynamic-slice_fusion.3
  103.4 1.6 %fusion.51 = (f32[2,4,256]{2,1,0:T(4,128)S(1)}, f32[2,256,256,4]{2,1,3,0:T(8,128)S(1)}) fusion(pred[256,256]{0,1:T(8,128)(4,1)S(1)} %compare_and_fusion.3, bf16[256,2,128,1]{0,2,3,1:T(8,128)(2,1)S(1)} %bitcast.121, bf16[256,2,4,128]{3,0,2,1:T(8,128)(2,1)} %get-tuple-element.537), kind=kOutput, calls=%fused_computation.3.clone.1 | convolution fusion | flops 135788544 | bytes 2826240 | tf_op jit(solution)/shard_map/while/body/eval_jaxpr/qgeh,kgh->geqk/dot_general | solution.py:36
  105.1 0.8 fusion.54
  106.7 1.0 constant_dynamic-slice_fusion.3
  107.8 1.6 %fusion.51 = (f32[2,4,256]{2,1,0:T(4,128)S(1)}, f32[2,256,256,4]{2,1,3,0:T(8,128)S(1)}) fusion(pred[256,256]{0,1:T(8,128)(4,1)S(1)} %compare_and_fusion.3, bf16[256,2,128,1]{0,2,3,1:T(8,128)(2,1)S(1)} %bitcast.121, bf16[256,2,4,128]{3,0,2,1:T(8,128)(2,1)} %get-tuple-element.537), kind=kOutput, calls=%fused_computation.3.clone.1 | convolution fusion | flops 135788544 | bytes 2826240 | tf_op jit(solution)/shard_map/while/body/eval_jaxpr/qgeh,kgh->geqk/dot_general | solution.py:36
  109.5 0.8 fusion.54
  110.3 0.5 fusion.53
  111.7 11.5 %all_to_all.56 = bf16[4,1,64,1024]{3,2,1,0:T(8,128)(2,1)S(1)} all-to-all(bf16[4,1,64,1024]{3,2,1,0:T(8,128)(2,1)S(1)} %pad_maximum_fusion.2), channel_id=1, replica_groups=mesh['head'=4,'outer'=2,'inner'=4] {'head'}, dimensions={0} | all-to-all | bytes 1048576 | tf_op jit(solution)/shard_map/all_to_all | solution.py:99
  123.3 0.8 copy.146
  (81 shorter events, 7.9 us)
Async XLA Ops:
  0.0 8.2 %copy-start = (bf16[1,64,4096]{2,1,0:T(8,128)(2,1)S(1)}, bf16[1,64,4096]{2,1,0:T(8,128)(2,1)}, u32[]{:S(2)}) copy-start(bf16[1,64,4096]{2,1,0:T(8,128)(2,1)} %param.6) | copy-start | bytes 1572868
  4.8 33.8 %all-to-all-start = ((bf16[4,2,8192]{2,1,0:T(2,128)(2,1)}), bf16[4,2,8192]{2,1,0:T(2,128)(2,1)S(1)}, u32[]{:S(2)}, u32[]{:S(2)}) async-start(bf16[4,2,8192]{2,1,0:T(2,128)(2,1)} %reshape.236), calls=%async_computation | async-start | bytes 262144 | tf_op jit(solution)/shard_map/all_to_all | solution.py:54
  11.0 23.9 %copy-start.1 = (bf16[1,64,1024]{2,1,0:T(8,128)(2,1)S(1)}, bf16[1,64,1024]{2,1,0:T(8,128)(2,1)}, u32[]{:S(2)}) copy-start(bf16[1,64,1024]{2,1,0:T(8,128)(2,1)} %param.8) | copy-start | bytes 393220
  33.4 5.0 %copy-start.3 = (s32[4]{0:T(128)S(1)}, s32[4]{0:T(128)}, u32[]{:S(2)}) copy-start(s32[4]{0:T(128)} %param.9) | copy-start | bytes 52
  38.7 7.9 %all-to-all-start.2 = ((bf16[4,2,8192]{2,1,0:T(2,128)(2,1)}), bf16[4,2,8192]{2,1,0:T(2,128)(2,1)S(1)}, u32[]{:S(2)}, u32[]{:S(2)}) async-start(bf16[4,2,8192]{2,1,0:T(2,128)(2,1)} %reshape.240), calls=%async_computation.2 | async-start | bytes 262144 | tf_op jit(solution)/shard_map/all_to_all | solution.py:55
  46.6 21.2 %all-to-all-start.1 = ((bf16[4,2,32768]{2,1,0:T(2,128)(2,1)}), bf16[4,2,32768]{2,1,0:T(2,128)(2,1)S(1)}, u32[]{:S(2)}, u32[]{:S(2)}) async-start(bf16[4,2,32768]{2,1,0:T(2,128)(2,1)} %reshape.238), calls=%async_computation.1 | async-start | bytes 1048576 | tf_op jit(solution)/shard_map/all_to_all | solution.py:53
  50.8 10.5 %collective-permute-start.1 = (bf16[1,256,256]{2,1,0:T(8,128)(2,1)S(1)}, bf16[1,256,256]{2,1,0:T(8,128)(2,1)S(1)}, u32[]{:S(2)}, u32[]{:S(2)}) collective-permute-start(bf16[1,256,256]{2,1,0:T(8,128)(2,1)S(1)} %bitcast.133), channel_id=1, source_target_pairs={{0,1},{1,2},{2,3},{3,4},{4,5},{5,6},{6,7},{8,9},{9,10},{10,11},{11... | collective-permute-start | bytes 393224 | tf_op jit(solution)/shard_map/ppermute | solution.py:15
  54.3 10.8 %collective-permute-start.4 = (bf16[1,256,256]{2,1,0:T(8,128)(2,1)S(1)}, bf16[1,256,256]{2,1,0:T(8,128)(2,1)S(1)}, u32[]{:S(2)}, u32[]{:S(2)}) collective-permute-start(bf16[1,256,256]{2,1,0:T(8,128)(2,1)S(1)} %bitcast.137), channel_id=1, source_target_pairs={{0,1},{1,2},{2,3},{3,4},{4,5},{5,6},{6,7},{8,9},{9,10},{10,11},{11... | collective-permute-start | bytes 393224 | tf_op jit(solution)/shard_map/ppermute | solution.py:15
  58.7 16.3 %collective-permute-start = (bf16[1,256,256]{2,1,0:T(8,128)(2,1)S(1)}, bf16[1,256,256]{2,1,0:T(8,128)(2,1)}, u32[]{:S(2)}, u32[]{:S(2)}) collective-permute-start(bf16[1,256,256]{2,1,0:T(8,128)(2,1)S(1)} %bitcast.134), channel_id=1, source_target_pairs={{0,4},{1,5},{2,6},{3,7},{8,12},{9,13},{10,14},{11,15},{16,20},{17,... | collective-permute-start | bytes 393224 | tf_op jit(solution)/shard_map/ppermute | solution.py:15
  60.0 28.5 %collective-permute-start.3 = (bf16[1,256,256]{2,1,0:T(8,128)(2,1)S(1)}, bf16[1,256,256]{2,1,0:T(8,128)(2,1)S(1)}, u32[]{:S(2)}, u32[]{:S(2)}) collective-permute-start(bf16[1,256,256]{2,1,0:T(8,128)(2,1)S(1)} %bitcast.138), channel_id=1, source_target_pairs={{0,4},{1,5},{2,6},{3,7},{8,12},{9,13},{10,14},{11,15},{16,20},{17,... | collective-permute-start | bytes 393224 | tf_op jit(solution)/shard_map/ppermute | solution.py:15
  62.1 24.6 %collective-permute-start.2 = (bf16[2,256,256]{2,1,0:T(8,128)(2,1)}, bf16[2,256,256]{2,1,0:T(8,128)(2,1)}, u32[]{:S(2)}, u32[]{:S(2)}) collective-permute-start(bf16[2,256,256]{2,1,0:T(8,128)(2,1)} %pad_maximum_fusion.3), channel_id=1, source_target_pairs={{0,2},{1,3},{2,4},{3,5},{4,6},{5,7},{8,10},{9,11},{10,12},{11,13},... | collective-permute-start | bytes 786440 | tf_op jit(solution)/shard_map/ppermute | solution.py:15
  65.9 25.5 %collective-permute-start.5 = (bf16[2,256,256]{2,1,0:T(8,128)(2,1)}, bf16[2,256,256]{2,1,0:T(8,128)(2,1)}, u32[]{:S(2)}, u32[]{:S(2)}) collective-permute-start(bf16[2,256,256]{2,1,0:T(8,128)(2,1)} %pad_maximum_fusion.4), channel_id=1, source_target_pairs={{0,2},{1,3},{2,4},{3,5},{4,6},{5,7},{8,10},{9,11},{10,12},{11,13},... | collective-permute-start | bytes 786440 | tf_op jit(solution)/shard_map/ppermute | solution.py:15
  71.9 1.0 copy-start.2
